TPU v7x, 128 devices: a whole 4x4x4 slice. The times are simulated.
128 devices in a mesh: area: 32 (over z_hi, x, y), inarea: 4 (over z_lo, core).
Axes of the slice: x: 4, y: 4, z: 4 (z_hi: 2, z_lo: 2; z = z_hi * 2 + z_lo), core: 2. Of those that a mesh axis runs over, the one named last changes fastest.
Arguments:
- spikes: int32 [2, 8, 65536], P(None, None, ('area', 'inarea')), may hold values 0 or 1
- release: float32 [8, 65536], P(None, ('area', 'inarea')), may hold values from 0.2 to 1
- potential: float32 [8, 65536], P(None, ('area', 'inarea')), may hold values from -6 to 6
- pre_trace: float32 [8, 65536], P(None, ('area', 'inarea')), may hold values from 0 to 2
- post_trace: float32 [8, 65536], P(None, ('area', 'inarea')), may hold values from 0 to 2
- w_local: float32 [65536, 2048], P(('area', 'inarea')), may hold values from -0.125 to 0.125
- w_long: float32 [65536, 3072], P(('area', 'inarea')), may hold values from -0.109375 to 0.109375
- sources: int32 [32, 12], replicated, may hold values from 0 to 255, as said below
- counts: int32 [32], replicated, may hold values from 512 to 2048, as said below
Outputs:
- voltage: float32 [8, 65536], P(None, ('area', 'inarea'))
- volley: float32 [8, 65536], P(None, ('area', 'inarea'))
- presyn: float32 [8, 65536], P(None, ('area', 'inarea'))
- postsyn: float32 [8, 65536], P(None, ('area', 'inarea'))
- local_new: float32 [65536, 2048], P(('area', 'inarea'))
- long_new: float32 [65536, 3072], P(('area', 'inarea'))
Inputs may be any that keep to these rules, and one draw needn't show every extreme that they name: `sources`: no area takes a block of its own; the 12 blocks of one area lie in 12 different runs of 2 blocks that start at multiples of 2. `counts`: some area is full in every draw.
All inputs are finite; a program needn't handle non-finite values. No bound on the sum of `spikes` on one device may be relied on, other than what follows from the above.
Results may differ from a plain program's by a relative error of at most 0.0001.
Values sent between devices are 32-bit elements; how exact they have to be, the bound alone decides.
A program may use at most 128 MiB of HBM per device.

v0:
```python
import functools

import jax
import jax.numpy as jnp
from jax import lax
from jax.experimental import pallas as pl
from jax.experimental.pallas import tpu as pltpu
from jax.sharding import PartitionSpec as P

MESH = pl.DeviceIdType.MESH
BLOCK = 256
SLOTS = 12
TRIALS = 8
OWN = 512
AREA = 2048
FAR = SLOTS * BLOCK
ROWS = 128

pre_decay = 0.8
postsyn_trace_decay = 0.7
leak_factor = 0.9
adaptation_speed = 0.0005
recovery = 0.2
depletion = 0.5

AXES = (("x", "y", "z"), ("y", "z", "x"), ("z", "x", "y"))
OFFSETS = (1, 3, 2)


def device_of(place):
    area = lax.div(place["z"], 2) * 16 + place["x"] * 4 + place["y"]
    return (area, lax.rem(place["z"], 2) * 2 + place["c"])


def my_place():
    area, inner = lax.axis_index("area"), lax.axis_index("inarea")
    return {
        "x": lax.rem(lax.div(area, 4), 4),
        "y": lax.rem(area, 4),
        "z": lax.div(area, 16) * 2 + lax.div(inner, 2),
        "c": lax.rem(inner, 2),
    }


def moved(place, axis, offset):
    return {**place, axis: lax.rem(place[axis] + offset, 4)}


def remote(src, dst, send_sem, recv_sem, device):
    return pltpu.make_async_remote_copy(
        src_ref=src,
        dst_ref=dst,
        send_sem=send_sem,
        recv_sem=recv_sem,
        device_id=device,
        device_id_type=MESH,
    )


def early_dynamics(spikes, release, pre_trace, alive):
    firing_1 = spikes[0].astype(jnp.float32) * alive
    activity_1 = firing_1 * release
    presyn_1 = (pre_decay * pre_trace + activity_1) * alive
    volley_1 = release + recovery * (1.0 - release) - depletion * activity_1
    firing_2 = spikes[1].astype(jnp.float32) * alive
    activity_2 = firing_2 * volley_1
    return firing_1, activity_1, presyn_1, volley_1, firing_2, activity_2


def alive_of(counts_ref):
    area, inner = lax.axis_index("area"), lax.axis_index("inarea")
    position = inner * OWN + lax.broadcasted_iota(jnp.int32, (TRIALS, OWN), 1)
    return jnp.where(position < counts_ref[area], 1.0, 0.0).astype(jnp.float32)


def exchange_kernel(
    sources_ref, counts_ref, spikes_hbm, release_hbm, pre_hbm, w_local_hbm, w_long_hbm,
    near_ref, far_ref, w_local_ref, w_long_ref,
    spikes_ref, release_ref, pre_ref, gathered_0, gathered_1, gathered_2, staged, landed_0, landed_1, landed_2,
    load_sem, weight_sem, near_send, near_recv, send_1, recv_1, pair_send, pair_recv,
    send_2, recv_2, send_3, recv_3, send_4, recv_4,
):
    here = my_place()
    inner = lax.axis_index("inarea")
    core = here["c"]
    sibling = {**here, "c": 1 - core}
    gathered = (gathered_0, gathered_1, gathered_2)
    landed = (landed_0, landed_1, landed_2)

    loads = [
        pltpu.make_async_copy(spikes_hbm, spikes_ref, load_sem.at[0]),
        pltpu.make_async_copy(release_hbm, release_ref, load_sem.at[1]),
        pltpu.make_async_copy(pre_hbm, pre_ref, load_sem.at[2]),
    ]
    for load in loads:
        load.start()
    weights = [
        pltpu.make_async_copy(w_local_hbm, w_local_ref, weight_sem.at[0]),
        pltpu.make_async_copy(w_long_hbm, w_long_ref, weight_sem.at[1]),
    ]
    for load in weights:
        load.start()

    barrier = pltpu.get_barrier_semaphore()
    partners = [sibling]
    for axis in "xyz":
        for offset in (1, 2, 3):
            there = moved(here, axis, offset)
            partners += [there, {**there, "c": 1 - core}]
    for partner in partners:
        pl.semaphore_signal(barrier, inc=1, device_id=device_of(partner), device_id_type=MESH)

    for load in loads:
        load.wait()
    _, activity_1, presyn_1, _, _, activity_2 = early_dynamics(
        spikes_ref[...], release_ref[...], pre_ref[...], alive_of(counts_ref)
    )
    for kind, value in enumerate((activity_1, presyn_1, activity_2)):
        for half in range(2):
            for block in range(2):
                column = block * BLOCK + half * 128
                near_ref[inner, kind, half, block] = value[:, column : column + 128]
    for kind, (first, second, _) in enumerate(AXES):
        gathered[kind][here[second], here[first], core] = near_ref[inner, kind, core]
    pl.semaphore_wait(barrier, len(partners))

    steps_1 = []
    for kind, (first, second, _) in enumerate(AXES):
        target = gathered[kind].at[here[second], here[first], core]
        copies = [
            remote(
                near_ref.at[inner, kind, 1 - core], target, pair_send.at[kind], pair_recv.at[kind],
                device_of(sibling),
            )
        ]
        for j, offset in enumerate(OFFSETS):
            for other in range(2):
                half = core if other == 0 else 1 - core
                copies.append(
                    remote(
                        near_ref.at[inner, kind, half], target,
                        send_1.at[kind, j, other], recv_1.at[kind, j, other],
                        device_of({**moved(here, first, offset), "c": half}),
                    )
                )
        steps_1.append(copies)
    for copies in zip(*steps_1):
        for copy in copies:
            copy.start()
    near_copies = []
    for flip in range(1, 4):
        z = here["z"] if flip < 2 else here["z"] + 1 - 2 * lax.rem(here["z"], 2)
        c = core if flip == 2 else 1 - core
        near_copies.append(
            remote(
                near_ref.at[inner], near_ref.at[inner], near_send.at[flip - 1], near_recv.at[flip - 1],
                device_of({**here, "z": z, "c": c}),
            )
        )
    for copy in near_copies:
        copy.start()

    steps_2 = []
    for kind, (first, second, _) in enumerate(AXES):
        for copy in steps_1[kind]:
            copy.wait_recv()
        copies = [
            remote(
                gathered[kind].at[here[second]], gathered[kind].at[here[second]],
                send_2.at[kind, j], recv_2.at[kind, j], device_of(moved(here, second, offset)),
            )
            for j, offset in enumerate(OFFSETS)
        ]
        for copy in copies:
            copy.start()
        steps_2.append(copies)

    def source_place(area, slot):
        block = sources_ref[area, slot]
        run = lax.shift_right_logical(block, 1)
        return {
            "b": block & 1,
            "c": run & 1,
            "x": lax.shift_right_logical(run, 4) & 3,
            "y": lax.shift_right_logical(run, 2) & 3,
            "z": lax.shift_right_logical(run, 6) * 2 + (lax.shift_right_logical(run, 1) & 1),
        }

    def pick(kind, area, slot):
        source = source_place(area, slot)
        first, second, _ = AXES[kind]
        return gathered[kind][source[second], source[first], source["c"], source["b"]]

    steps_3 = []
    for kind, (_, _, third) in enumerate(AXES):
        for copy in steps_2[kind]:
            copy.wait_recv()
        copies = []
        for j, offset in enumerate(OFFSETS):
            there = moved(here, third, offset)
            area, _ = device_of(there)
            for slot in range(SLOTS):
                staged[kind, j, slot] = pick(kind, area, slot)
            copy = remote(
                staged.at[kind, j], landed[kind].at[here[third]],
                send_3.at[kind, j], recv_3.at[kind, j], device_of(there),
            )
            copy.start()
            copies.append(copy)
        steps_3.append(copies)
        for slot in range(SLOTS):
            landed[kind][here[third], slot] = pick(kind, lax.axis_index("area"), slot)

    steps_4 = []
    for kind, (_, _, third) in enumerate(AXES):
        for copy in steps_3[kind]:
            copy.wait_recv()
        for slot in range(SLOTS):
            plane = source_place(lax.axis_index("area"), slot)[third]
            far_ref[kind, core, slot] = landed[kind][plane, slot]
        copy = remote(
            far_ref.at[kind, core], far_ref.at[kind, core],
            send_4.at[kind], recv_4.at[kind], device_of(sibling),
        )
        copy.start()
        steps_4.append(copy)

    for copy in near_copies + steps_4:
        copy.wait_recv()
    for copies in steps_1 + steps_2 + steps_3 + [near_copies, steps_4]:
        for copy in copies:
            copy.wait_send()
    for load in weights:
        load.wait()


def split(value):
    high = value.astype(jnp.bfloat16)
    return high, (value - high.astype(jnp.float32)).astype(jnp.bfloat16)


def dot(a, b):
    return lax.dot_general(a, b, (((1,), (0,)), ((), ())), preferred_element_type=jnp.float32)


def synapse_kernel(
    counts_ref, near_ref, far_ref, w_local_ref, w_long_ref,
    spikes_ref, release_ref, potential_ref, pre_ref, post_ref,
    voltage_ref, volley_ref, presyn_ref, postsyn_ref, local_hbm, long_hbm,
    local_out, long_out, right_ref, act_ref, left_ref, current_ref, out_sem,
):
    alive = alive_of(counts_ref)
    firing_1, activity_1, presyn_1, volley_1, firing_2, activity_2 = early_dynamics(
        spikes_ref[...], release_ref[...], pre_ref[...], alive
    )
    post_1 = post_ref[...]
    post_2 = (postsyn_trace_decay * post_1 + firing_1) * alive
    presyn_ref[...] = (pre_decay * presyn_1 + activity_2) * alive
    postsyn_ref[...] = (postsyn_trace_decay * post_2 + firing_2) * alive
    volley_ref[...] = volley_1 + recovery * (1.0 - volley_1) - depletion * activity_2

    def high(value):
        return value.astype(jnp.bfloat16).astype(jnp.float32)

    minus_1, minus_2 = -post_1, -post_2
    left = jnp.concatenate(
        [
            firing_1, firing_1, firing_2, firing_2,
            high(minus_1), high(minus_1), minus_1 - high(minus_1),
            high(minus_2), high(minus_2), minus_2 - high(minus_2),
        ],
        axis=0,
    )
    left_ref[...] = left.T.astype(jnp.bfloat16)

    def sent(kind):
        near = [near_ref[i, kind, h, b] for i in range(4) for b in range(2) for h in range(2)]
        far = [far_ref[kind, h, s] for s in range(SLOTS) for h in range(2)]
        return jnp.concatenate(near + far, axis=1)

    act_1, pre_1, act_2 = sent(0), sent(1), sent(2)
    pre_2 = pre_decay * pre_1 + act_2
    parts = []
    for value in (pre_1, pre_2):
        big = high(adaptation_speed * value)
        parts += [big, adaptation_speed * value - big]
    for value in (act_1, act_2):
        big = high(adaptation_speed * value)
        parts += [big, adaptation_speed * value - big, big]
    right_ref[...] = jnp.concatenate(parts, axis=0).astype(jnp.bfloat16)

    both = jnp.concatenate([act_1, act_2], axis=0)
    big = high(both)
    act_ref[...] = jnp.concatenate([big, both - big], axis=0).T.astype(jnp.bfloat16)
    cross_high, cross_low = split(jnp.concatenate([pre_1, act_1], axis=0))
    cross = dot(cross_high, act_ref[...]) + dot(cross_low, act_ref[...])
    cross = adaptation_speed * (cross[:, 8:16] + cross[:, 24:32])

    def out_copies(step):
        rows = pl.ds(pl.multiple_of(step * ROWS, ROWS), ROWS)
        return (
            pltpu.make_async_copy(local_out.at[rows], local_hbm.at[rows], out_sem.at[0, step]),
            pltpu.make_async_copy(long_out.at[rows], long_hbm.at[rows], out_sem.at[1, step]),
        )

    @pl.loop(0, OWN // ROWS)
    def _(step):
        rows = pl.ds(pl.multiple_of(step * ROWS, ROWS), ROWS)
        w_near, w_far = w_local_ref[rows, :], w_long_ref[rows, :]
        near_high, near_low = split(w_near)
        far_high, far_low = split(w_far)
        current_ref[rows, :] = (
            dot(near_high, act_ref[:AREA, :]) + dot(near_low, act_ref[:AREA, :])
            + dot(far_high, act_ref[AREA:, :]) + dot(far_low, act_ref[AREA:, :])
        )
        local_out[rows, :] = w_near + dot(left_ref[rows, :], right_ref[:, :AREA])
        long_out[rows, :] = w_far + dot(left_ref[rows, :], right_ref[:, AREA:])
        for copy in out_copies(step):
            copy.start()

    current = current_ref[...].T
    current_1 = current[0:8] + current[16:24]
    current_2 = current[8:16] + current[24:32]
    extra = lax.dot_general(
        cross, jnp.concatenate([firing_1, -post_1], axis=0), (((0,), (0,)), ((), ())),
        preferred_element_type=jnp.float32, precision=lax.Precision.HIGHEST,
    )
    voltage_1 = (leak_factor * potential_ref[...] + current_1) * alive
    voltage_ref[...] = (leak_factor * voltage_1 + (current_2 + extra)) * alive

    @pl.loop(0, OWN // ROWS)
    def _(step):
        for copy in out_copies(step):
            copy.wait()


def local(spikes, release, potential, pre_trace, post_trace, w_local, w_long, sources, counts):
    smem = pl.BlockSpec(memory_space=pltpu.SMEM)
    hbm = pl.BlockSpec(memory_space=pltpu.HBM)
    vmem = pl.BlockSpec(memory_space=pltpu.VMEM)
    dma = pltpu.SemaphoreType.DMA
    f32 = jnp.float32
    in_hbm = functools.partial(pltpu.with_memory_space_constraint, memory_space=pltpu.HBM)
    near, far, w_local_in, w_long_in = pl.pallas_call(
        exchange_kernel,
        name="exchange",
        out_shape=(
            pltpu.VMEM((4, 3, 2, 2, TRIALS, 128), f32),
            pltpu.VMEM((3, 2, SLOTS, TRIALS, 128), f32),
            pltpu.VMEM((OWN, AREA), f32),
            pltpu.VMEM((OWN, FAR), f32),
        ),
        in_specs=[smem, smem, hbm, hbm, hbm, hbm, hbm],
        out_specs=(vmem, vmem, vmem, vmem),
        scratch_shapes=[
            pltpu.VMEM((2, TRIALS, OWN), jnp.int32),
            pltpu.VMEM((TRIALS, OWN), f32),
            pltpu.VMEM((TRIALS, OWN), f32),
            *[pltpu.VMEM((4, 4, 2, 2, TRIALS, 128), f32)] * 3,
            pltpu.VMEM((3, 3, SLOTS, TRIALS, 128), f32),
            *[pltpu.VMEM((4, SLOTS, TRIALS, 128), f32)] * 3,
            dma((3,)), dma((2,)), dma((3,)), dma((3,)),
            dma((3, 3, 2)), dma((3, 3, 2)), dma((3,)), dma((3,)),
            dma((3, 3)), dma((3, 3)), dma((3, 3)), dma((3, 3)), dma((3,)), dma((3,)),
        ],
        compiler_params=pltpu.CompilerParams(
            collective_id=0, has_side_effects=True, vmem_limit_bytes=20 << 20
        ),
    )(sources, counts, *(in_hbm(x) for x in (spikes, release, pre_trace, w_local, w_long)))

    columns = AREA + FAR
    return pl.pallas_call(
        synapse_kernel,
        name="synapses",
        out_shape=(
            *(jax.ShapeDtypeStruct((TRIALS, OWN), f32) for _ in range(4)),
            jax.ShapeDtypeStruct((OWN, AREA), f32),
            jax.ShapeDtypeStruct((OWN, FAR), f32),
        ),
        in_specs=[smem] + [vmem] * 9,
        out_specs=(vmem, vmem, vmem, vmem, hbm, hbm),
        scratch_shapes=[
            pltpu.VMEM((OWN, AREA), f32),
            pltpu.VMEM((OWN, FAR), f32),
            pltpu.VMEM((80, columns), jnp.bfloat16),
            pltpu.VMEM((columns, 32), jnp.bfloat16),
            pltpu.VMEM((OWN, 80), jnp.bfloat16),
            pltpu.VMEM((OWN, 32), f32),
            dma((2, OWN // ROWS)),
        ],
        compiler_params=pltpu.CompilerParams(vmem_limit_bytes=40 << 20),
    )(counts, near, far, w_local_in, w_long_in, spikes, release, potential, pre_trace, post_trace)


def solution(mesh):
    neurons = P(None, ("area", "inarea"))
    synapses = P(("area", "inarea"), None)
    return jax.shard_map(
        local,
        mesh=mesh,
        in_specs=(
            P(None, None, ("area", "inarea")), neurons, neurons, neurons, neurons,
            synapses, synapses, P(), P(),
        ),
        out_specs=(neurons, neurons, neurons, neurons, synapses, synapses),
        check_vma=False,
    )
```

profile of v0, /device:TPU:1, one launch (start us, length us, event | category | flops | bytes accessed | tf_op | source)
XLA Modules:
  0.0 35.5 jit_solution(13986642879461034892)
XLA Ops:
  0.6 0.0 copy-start.2
  0.6 0.0 copy-start.1
  0.7 0.0 copy-start
  0.7 0.0 copy-start.4
  0.7 0.0 copy-start.3
  0.7 0.8 %copy.15.sources_ref = s32[32,12]{1,0:T(8,128)S(1)} copy(s32[32,12]{0,1:T(8,128)} %param.16) | data formatting | bytes 3072 | tf_op args[7]
  1.5 0.0 copy-start.5
  1.5 0.7 %copy-done.5 = s32[32]{0:T(128)S(1)} copy-done((s32[32]{0:T(128)S(1)}, s32[32]{0:T(128)}, u32[]{:S(2)}) %copy-start.5) | copy-done | bytes 152
  2.1 24.8 %exchange.1 = (f32[4,3,2,2,8,128]{5,4,3,2,1,0:T(8,128)S(1)}, f32[3,2,12,8,128]{4,3,2,1,0:T(8,128)S(1)}, f32[512,2048]{1,0:T(8,128)S(1)}, f32[512,3072]{1,0:T(8,128)S(1)}) custom-call(s32[32,12]{1,0:T(8,128)S(1)} %copy.15.sources_ref, s32[32]{0:T(128)S(1)} %copy-done.5, s32[2,8,512]{2,1,0:T(8,128)} %spikes_ref.1, f32[8,512]{1,0:T(8,128)} %release_ref.1, ...), custom_call_target="tpu_custom_call" | custom-call | tf_op jit(solution)/shard_map/exchange/pallas_call | solution.py:344
  26.9 0.0 copy-done.2
  26.9 0.0 copy-done.1
  26.9 0.0 copy-done
  26.9 0.0 copy-done.4
  26.9 0.0 copy-done.3
  27.0 8.6 %synapses.1 = (f32[8,512]{1,0:T(8,128)}, f32[8,512]{1,0:T(8,128)}, f32[8,512]{1,0:T(8,128)}, f32[8,512]{1,0:T(8,128)}, f32[512,2048]{1,0:T(8,128)}, /*index=5*/f32[512,3072]{1,0:T(8,128)}) custom-call(s32[32]{0:T(128)S(1)} %copy-done.5, f32[4,3,2,2,8,128]{5,4,3,2,1,0:T(8,128)S(1)} %get-tuple-element.10.near_ref, ...), custom_call_target="tpu_custom_call" | custom-call | tf_op jit(solution)/shard_map/synapses/pallas_call | solution.py:372
Async XLA Ops:
  0.6 26.3 %copy-start.2 = (f32[8,512]{1,0:T(8,128)S(1)}, f32[8,512]{1,0:T(8,128)}, u32[]{:S(2)}) copy-start(f32[8,512]{1,0:T(8,128)} %pre_ref.1) | copy-start | bytes 49156
  0.6 26.3 %copy-start.1 = (f32[8,512]{1,0:T(8,128)S(1)}, f32[8,512]{1,0:T(8,128)}, u32[]{:S(2)}) copy-start(f32[8,512]{1,0:T(8,128)} %release_ref.1) | copy-start | bytes 49156
  0.7 26.3 %copy-start = (s32[2,8,512]{2,1,0:T(8,128)S(1)}, s32[2,8,512]{2,1,0:T(8,128)}, u32[]{:S(2)}) copy-start(s32[2,8,512]{2,1,0:T(8,128)} %spikes_ref.1) | copy-start | bytes 98308
  0.7 26.3 %copy-start.4 = (f32[8,512]{1,0:T(8,128)S(1)}, f32[8,512]{1,0:T(8,128)}, u32[]{:S(2)}) copy-start(f32[8,512]{1,0:T(8,128)} %post_ref.1) | copy-start | bytes 49156
  0.7 26.3 %copy-start.3 = (f32[8,512]{1,0:T(8,128)S(1)}, f32[8,512]{1,0:T(8,128)}, u32[]{:S(2)}) copy-start(f32[8,512]{1,0:T(8,128)} %potential_ref.1) | copy-start | bytes 49156
  1.5 0.7 %copy-start.5 = (s32[32]{0:T(128)S(1)}, s32[32]{0:T(128)}, u32[]{:S(2)}) copy-start(s32[32]{0:T(128)} %counts_ref.3) | copy-start | bytes 388
where the time goes:
time: 35.7 us; the launch traced here: 35.5 us
  Pallas kernels  33.3 us (93%)
  local copies, waits for them, and re-layouts  1.48 us (4%)
  between operations  0.72 us (2%)
    pallas_call x1, Pallas kernels, local(): pl.pallas_call(exchange_kernel, name='exchange', out_shape=(pltpu.VMEM((4...  24.8 us
    pallas_call x1, Pallas kernels, local(): pl.pallas_call(synapse_kernel, name='synapses', out_shape=(*(jax.ShapeDty...  8.58 us
    unnamed x13, local copies, waits for them, and re-layouts  1.48 us

commit v1 on v0

v1 whole, which is shorter than its diff:
```python
import functools

import jax
import jax.numpy as jnp
from jax import lax
from jax.experimental import pallas as pl
from jax.experimental.pallas import tpu as pltpu
from jax.sharding import PartitionSpec as P

MESH = pl.DeviceIdType.MESH
BLOCK = 256
SLOTS = 12
TRIALS = 8
OWN = 512
AREA = 2048
FAR = SLOTS * BLOCK
ROWS = 128
TILE = (TRIALS, 128)

pre_decay = 0.8
postsyn_trace_decay = 0.7
leak_factor = 0.9
adaptation_speed = 0.0005
recovery = 0.2
depletion = 0.5

AXES = (("x", "y", "z"), ("y", "z", "x"), ("z", "x", "y"))
OFFSETS = (1, 3, 2)


def device_of(place):
    area = lax.div(place["z"], 2) * 16 + place["x"] * 4 + place["y"]
    return (area, lax.rem(place["z"], 2) * 2 + place["c"])


def my_place():
    area, inner = lax.axis_index("area"), lax.axis_index("inarea")
    return {
        "x": lax.rem(lax.div(area, 4), 4),
        "y": lax.rem(area, 4),
        "z": lax.div(area, 16) * 2 + lax.div(inner, 2),
        "c": lax.rem(inner, 2),
    }


def moved(place, axis, offset):
    return {**place, axis: lax.rem(place[axis] + offset, 4)}


def remote(src, dst, send_sem, recv_sem, device):
    return pltpu.make_async_remote_copy(
        src_ref=src,
        dst_ref=dst,
        send_sem=send_sem,
        recv_sem=recv_sem,
        device_id=device,
        device_id_type=MESH,
    )


def early_dynamics(spikes, release, pre_trace, alive):
    firing_1 = spikes[0].astype(jnp.float32) * alive
    activity_1 = firing_1 * release
    presyn_1 = (pre_decay * pre_trace + activity_1) * alive
    volley_1 = release + recovery * (1.0 - release) - depletion * activity_1
    firing_2 = spikes[1].astype(jnp.float32) * alive
    activity_2 = firing_2 * volley_1
    return firing_1, activity_1, presyn_1, volley_1, firing_2, activity_2


def alive_of(counts_ref):
    area, inner = lax.axis_index("area"), lax.axis_index("inarea")
    position = inner * OWN + lax.broadcasted_iota(jnp.int32, (TRIALS, OWN), 1)
    return jnp.where(position < counts_ref[area], 1.0, 0.0).astype(jnp.float32)


def high(value):
    return value.astype(jnp.bfloat16).astype(jnp.float32)


def halves(value):
    big = high(value)
    return big, value - big


def dot(a, b):
    return lax.dot_general(a, b, (((1,), (0,)), ((), ())), preferred_element_type=jnp.float32)


def dot_t(a, b):
    return lax.dot_general(a, b, (((1,), (1,)), ((), ())), preferred_element_type=jnp.float32)


def left_matrix(firing_1, firing_2, post_1, post_2):
    big_1, small_1 = halves(-post_1)
    big_2, small_2 = halves(-post_2)
    parts = [firing_1, firing_1, firing_2, firing_2, big_1, big_1, small_1, big_2, big_2, small_2]
    return jnp.concatenate(parts, axis=0).T.astype(jnp.bfloat16)


def right_matrix(act_1, pre_1, act_2):
    parts = []
    for value in (pre_1, pre_decay * pre_1 + act_2):
        parts += halves(adaptation_speed * value)
    for value in (act_1, act_2):
        big, small = halves(adaptation_speed * value)
        parts += [big, small, big]
    return jnp.concatenate(parts, axis=0).astype(jnp.bfloat16)


def activity_matrix(act_1, act_2):
    return jnp.concatenate(halves(jnp.concatenate([act_1, act_2], axis=0)), axis=0).astype(jnp.bfloat16)


def cross_products(act_1, pre_1, activity):
    big, small = halves(jnp.concatenate([pre_1, act_1], axis=0))
    return dot_t(big.astype(jnp.bfloat16), activity) + dot_t(small.astype(jnp.bfloat16), activity)


def row_block(step, rows=ROWS):
    return pl.ds(pl.multiple_of(step * rows, rows), rows)


def exchange_kernel(
    sources_hbm, counts_hbm, spikes_hbm, release_hbm, pre_hbm, post_hbm, w_local_hbm, w_long_hbm,
    far_ref, local_ref, w_long_ref, high_ref, low_ref, left_ref, current_ref, cross_ref, alive_ref,
    sources_ref, counts_ref, index_ref,
    spikes_ref, release_ref, pre_ref, post_ref, near_ref, gathered_0, gathered_1, gathered_2, staged,
    landed_0, landed_1, landed_2, right_ref, activity_ref,
    load_sem, source_sem, weight_sem, near_recv, recv_1, recv_2, recv_3, recv_4, send_sem,
):
    here = my_place()
    inner = lax.axis_index("inarea")
    core = here["c"]
    sibling = {**here, "c": 1 - core}
    gathered = (gathered_0, gathered_1, gathered_2)
    landed = (landed_0, landed_1, landed_2)

    loads = [
        pltpu.make_async_copy(src, dst, load_sem.at[i])
        for i, (src, dst) in enumerate(
            (
                (counts_hbm, counts_ref), (spikes_hbm, spikes_ref), (release_hbm, release_ref),
                (pre_hbm, pre_ref), (post_hbm, post_ref),
            )
        )
    ]
    for load in loads:
        load.start()
    source_load = pltpu.make_async_copy(sources_hbm, sources_ref, source_sem)
    source_load.start()
    weight_loads = [
        pltpu.make_async_copy(w_long_hbm, w_long_ref, weight_sem.at[0]),
        pltpu.make_async_copy(w_local_hbm, local_ref, weight_sem.at[1]),
    ]
    for load in weight_loads:
        load.start()

    barrier = pltpu.get_barrier_semaphore()
    partners = [sibling]
    for axis in "xyz":
        for offset in (1, 2, 3):
            there = moved(here, axis, offset)
            partners += [there, {**there, "c": 1 - core}]
    for partner in partners:
        pl.semaphore_signal(barrier, inc=1, device_id=device_of(partner), device_id_type=MESH)

    for load in loads:
        load.wait()
    alive = alive_of(counts_ref)
    firing_1, activity_1, presyn_1, _, firing_2, activity_2 = early_dynamics(
        spikes_ref[...], release_ref[...], pre_ref[...], alive
    )
    for kind, value in enumerate((activity_1, presyn_1, activity_2)):
        for half in range(2):
            for block in range(2):
                column = block * BLOCK + half * 128
                near_ref[inner * 12 + kind * 4 + half * 2 + block] = value[:, column : column + 128]

    def mine(kind, half):
        return pl.ds(inner * 12 + kind * 4 + half * 2, 2)

    spots = [here[second] * 16 + here[first] * 4 + core * 2 for first, second, _ in AXES]
    for kind in range(3):
        gathered[kind][pl.ds(spots[kind], 2)] = near_ref[mine(kind, core)]
    pl.semaphore_wait(barrier, len(partners))

    def arrived(ref, sem):
        pltpu.make_async_copy(ref, ref, sem).wait()

    def step_1(kind, place, half):
        remote(
            near_ref.at[mine(kind, half)], gathered[kind].at[pl.ds(spots[kind], 2)],
            send_sem.at[0], recv_1.at[kind], device_of({**place, "c": half}),
        ).start()

    for offset in OFFSETS:
        for kind, (first, _, _) in enumerate(AXES):
            there = moved(here, first, offset)
            step_1(kind, there, core)
            step_1(kind, there, 1 - core)
    for kind in range(3):
        step_1(kind, here, 1 - core)
    for flip in range(1, 4):
        z = here["z"] if flip < 2 else here["z"] + 1 - 2 * lax.rem(here["z"], 2)
        c = core if flip == 2 else 1 - core
        remote(
            near_ref.at[pl.ds(inner * 12, 12)], near_ref.at[pl.ds(inner * 12, 12)],
            send_sem.at[1], near_recv, device_of({**here, "z": z, "c": c}),
        ).start()

    source_load.wait()

    def note_indices(slot, area):
        block = sources_ref[slot, area]
        run = lax.shift_right_logical(block, 1)
        return {
            "cb": (run & 1) * 2 + (block & 1),
            "x": lax.shift_right_logical(run, 4) & 3,
            "y": lax.shift_right_logical(run, 2) & 3,
            "z": lax.shift_right_logical(run, 6) * 2 + (lax.shift_right_logical(run, 1) & 1),
        }

    def spot_of(kind, source):
        first, second, _ = AXES[kind]
        return source[second] * 16 + source[first] * 4 + source["cb"]

    @pl.loop(0, SLOTS)
    def _(slot):
        own = note_indices(slot, lax.axis_index("area"))
        for kind, (_, _, third) in enumerate(AXES):
            index_ref[kind * 5 + 3, slot] = spot_of(kind, own)
            index_ref[kind * 5 + 4, slot] = own[third] * SLOTS + slot
            for j, offset in enumerate(OFFSETS):
                area, _ = device_of(moved(here, third, offset))
                index_ref[kind * 5 + j, slot] = spot_of(kind, note_indices(slot, area))

    alive_ref[...] = alive
    post_1 = post_ref[...]
    post_2 = (postsyn_trace_decay * post_1 + firing_1) * alive
    left_ref[...] = left_matrix(firing_1, firing_2, post_1, post_2)
    weight_loads[0].wait()

    @pl.loop(0, OWN // 32)
    def _(step):
        rows = row_block(step, 32)
        value = w_long_ref[rows, :]
        big = value.astype(jnp.bfloat16)
        high_ref[rows, :] = big
        low_ref[rows, :] = (value - big.astype(jnp.float32)).astype(jnp.bfloat16)

    for kind, (first, second, _) in enumerate(AXES):
        arrived(gathered[kind].at[pl.ds(0, 14)], recv_1.at[kind])
        part = gathered[kind].at[pl.ds(here[second] * 16, 16)]
        for offset in OFFSETS:
            remote(
                part, part, send_sem.at[2], recv_2.at[kind], device_of(moved(here, second, offset))
            ).start()

    arrived(near_ref.at[pl.ds(0, 36)], near_recv)
    act_1, pre_1, act_2 = (
        jnp.concatenate(
            [near_ref[i * 12 + kind * 4 + h * 2 + b] for i in range(4) for b in range(2) for h in range(2)],
            axis=1,
        )
        for kind in range(3)
    )
    right_ref[...] = right_matrix(act_1, pre_1, act_2)
    activity_ref[...] = activity_matrix(act_1, act_2)
    cross_ref[...] = cross_products(act_1, pre_1, activity_ref[...])
    weight_loads[1].wait()

    @pl.loop(0, OWN // ROWS)
    def _(step):
        rows = row_block(step)
        value = local_ref[rows, :]
        big = value.astype(jnp.bfloat16)
        small = (value - big.astype(jnp.float32)).astype(jnp.bfloat16)
        current_ref[rows, :] = dot_t(big, activity_ref[...]) + dot_t(small, activity_ref[...])
        local_ref[rows, :] = value + dot(left_ref[rows, :], right_ref[...])

    for kind, (_, _, third) in enumerate(AXES):
        arrived(gathered[kind].at[pl.ds(0, 48)], recv_2.at[kind])
        for j, offset in enumerate(OFFSETS):
            first = (kind * 3 + j) * SLOTS
            for slot in range(SLOTS):
                staged[first + slot] = gathered[kind][index_ref[kind * 5 + j, slot]]
            remote(
                staged.at[pl.ds(first, SLOTS)], landed[kind].at[pl.ds(here[third] * SLOTS, SLOTS)],
                send_sem.at[3], recv_3.at[kind], device_of(moved(here, third, offset)),
            ).start()
        for slot in range(SLOTS):
            landed[kind][here[third] * SLOTS + slot] = gathered[kind][index_ref[kind * 5 + 3, slot]]

    for kind in range(3):
        arrived(landed[kind].at[pl.ds(0, 36)], recv_3.at[kind])
        first = kind * 24 + core * SLOTS
        for slot in range(SLOTS):
            far_ref[first + slot] = landed[kind][index_ref[kind * 5 + 4, slot]]
        part = far_ref.at[pl.ds(first, SLOTS)]
        remote(part, part, send_sem.at[4], recv_4, device_of(sibling)).start()

    arrived(far_ref.at[pl.ds(0, 36)], recv_4)
    for i, ref in enumerate(
        (
            gathered_0.at[pl.ds(0, 42)], near_ref.at[pl.ds(0, 36)], w_long_ref.at[pl.ds(0, 48)],
            staged, far_ref.at[pl.ds(0, 36)],
        )
    ):
        arrived(ref, send_sem.at[i])


def synapse_kernel(
    far_ref, local_ref, w_long_ref, high_ref, low_ref, left_ref, current_near, cross_near, alive_ref,
    spikes_ref, release_ref, potential_ref, pre_ref, post_ref,
    voltage_ref, volley_ref, presyn_ref, postsyn_ref, local_hbm, long_hbm,
    long_out, right_ref, activity_ref, current_ref, out_sem,
):
    local_copy = pltpu.make_async_copy(local_ref, local_hbm, out_sem.at[OWN // ROWS])
    local_copy.start()
    act_1, pre_1, act_2 = (
        jnp.concatenate([far_ref[kind * 24 + h * SLOTS + s] for s in range(SLOTS) for h in range(2)], axis=1)
        for kind in range(3)
    )
    right_ref[...] = right_matrix(act_1, pre_1, act_2)
    activity_ref[...] = activity_matrix(act_1, act_2)

    def long_copy(step):
        rows = row_block(step)
        return pltpu.make_async_copy(long_out.at[rows], long_hbm.at[rows], out_sem.at[step])

    @pl.loop(0, OWN // ROWS)
    def _(step):
        rows = row_block(step)
        long_out[rows, :] = w_long_ref[rows, :] + dot(left_ref[rows, :], right_ref[...])
        long_copy(step).start()

    @pl.loop(0, OWN // ROWS)
    def _(step):
        rows = row_block(step)
        current_ref[rows, :] = (
            current_near[rows, :]
            + dot_t(high_ref[rows, :], activity_ref[...]) + dot_t(low_ref[rows, :], activity_ref[...])
        )

    alive = alive_ref[...]
    firing_1, activity_1, presyn_1, volley_1, firing_2, activity_2 = early_dynamics(
        spikes_ref[...], release_ref[...], pre_ref[...], alive
    )
    post_1 = post_ref[...]
    post_2 = (postsyn_trace_decay * post_1 + firing_1) * alive
    presyn_ref[...] = (pre_decay * presyn_1 + activity_2) * alive
    postsyn_ref[...] = (postsyn_trace_decay * post_2 + firing_2) * alive
    volley_ref[...] = volley_1 + recovery * (1.0 - volley_1) - depletion * activity_2

    cross = cross_near[...] + cross_products(act_1, pre_1, activity_ref[...])
    cross = adaptation_speed * (cross[:, 8:16] + cross[:, 24:32])
    current = current_ref[...].T
    current_1 = current[0:8] + current[16:24]
    current_2 = current[8:16] + current[24:32]
    extra = lax.dot_general(
        cross, jnp.concatenate([firing_1, -post_1], axis=0), (((0,), (0,)), ((), ())),
        preferred_element_type=jnp.float32, precision=lax.Precision.HIGHEST,
    )
    voltage_1 = (leak_factor * potential_ref[...] + current_1) * alive
    voltage_ref[...] = (leak_factor * voltage_1 + (current_2 + extra)) * alive

    @pl.loop(0, OWN // ROWS)
    def _(step):
        long_copy(step).wait()
    local_copy.wait()


def local(spikes, release, potential, pre_trace, post_trace, w_local, w_long, sources, counts):
    hbm = pl.BlockSpec(memory_space=pltpu.HBM)
    vmem = pl.BlockSpec(memory_space=pltpu.VMEM)
    dma = pltpu.SemaphoreType.DMA
    f32, bf16 = jnp.float32, jnp.bfloat16
    in_hbm = functools.partial(pltpu.with_memory_space_constraint, memory_space=pltpu.HBM)
    parts = pl.pallas_call(
        exchange_kernel,
        name="exchange",
        out_shape=(
            pltpu.VMEM((72, *TILE), f32),
            pltpu.VMEM((OWN, AREA), f32),
            pltpu.VMEM((OWN, FAR), f32),
            pltpu.VMEM((OWN, FAR), bf16),
            pltpu.VMEM((OWN, FAR), bf16),
            pltpu.VMEM((OWN, 80), bf16),
            pltpu.VMEM((OWN, 32), f32),
            pltpu.VMEM((16, 32), f32),
            pltpu.VMEM((TRIALS, OWN), f32),
        ),
        in_specs=[hbm] * 8,
        out_specs=(vmem,) * 9,
        scratch_shapes=[
            pltpu.SMEM((SLOTS, 32), jnp.int32),
            pltpu.SMEM((32,), jnp.int32),
            pltpu.SMEM((15, SLOTS), jnp.int32),
            pltpu.VMEM((2, TRIALS, OWN), jnp.int32),
            *[pltpu.VMEM((TRIALS, OWN), f32)] * 3,
            pltpu.VMEM((48, *TILE), f32),
            *[pltpu.VMEM((64, *TILE), f32)] * 3,
            pltpu.VMEM((108, *TILE), f32),
            *[pltpu.VMEM((48, *TILE), f32)] * 3,
            pltpu.VMEM((80, AREA), bf16),
            pltpu.VMEM((32, AREA), bf16),
            dma((5,)), dma, dma((2,)), dma, dma((3,)), dma((3,)), dma((3,)), dma, dma((5,)),
        ],
        compiler_params=pltpu.CompilerParams(
            collective_id=0, has_side_effects=True, vmem_limit_bytes=28 << 20
        ),
    )(
        in_hbm(sources.T), in_hbm(counts),
        *(in_hbm(x) for x in (spikes, release, pre_trace, post_trace, w_local, w_long)),
    )
    return pl.pallas_call(
        synapse_kernel,
        name="synapses",
        out_shape=(
            *(jax.ShapeDtypeStruct((TRIALS, OWN), f32) for _ in range(4)),
            jax.ShapeDtypeStruct((OWN, AREA), f32),
            jax.ShapeDtypeStruct((OWN, FAR), f32),
        ),
        in_specs=[vmem] * 14,
        out_specs=(vmem, vmem, vmem, vmem, hbm, hbm),
        scratch_shapes=[
            pltpu.VMEM((OWN, FAR), f32),
            pltpu.VMEM((80, FAR), bf16),
            pltpu.VMEM((32, FAR), bf16),
            pltpu.VMEM((OWN, 32), f32),
            dma((OWN // ROWS + 1,)),
        ],
        compiler_params=pltpu.CompilerParams(vmem_limit_bytes=34 << 20),
    )(*parts, spikes, release, potential, pre_trace, post_trace)


def solution(mesh):
    neurons = P(None, ("area", "inarea"))
    synapses = P(("area", "inarea"), None)
    return jax.shard_map(
        local,
        mesh=mesh,
        in_specs=(
            P(None, None, ("area", "inarea")), neurons, neurons, neurons, neurons,
            synapses, synapses, P(), P(),
        ),
        out_specs=(neurons, neurons, neurons, neurons, synapses, synapses),
        check_vma=False,
    )
```

time: 35.7 us -> 30.6 us (0.86)
  Pallas kernels: 33.3 us -> 29.8 us
  local copies, waits for them, and re-layouts: 1.48 us -> 0.02 us
    pallas_call x1, Pallas kernels: 8.58 us -> 4.99 us  [local(): pl.pallas_call(synapse_kernel, name='synapses', out_shape=(*(jax.ShapeDty...]
    unnamed x13 -> x10, local copies, waits for them, and re-layouts: 1.48 us -> 0.02 us
where the time goes in v1:
time: 30.6 us; the launch traced here: 30.5 us
  Pallas kernels  29.8 us (97%)
  between operations  0.72 us (2%)
    pallas_call x1, Pallas kernels, local(): pl.pallas_call(exchange_kernel, name='exchange', out_shape=(pltpu.VMEM((7...  24.8 us
    pallas_call x1, Pallas kernels, local(): pl.pallas_call(synapse_kernel, name='synapses', out_shape=(*(jax.ShapeDty...  4.99 us

profile of v1, /device:TPU:1, one launch (start us, length us, event | category | flops | bytes accessed | tf_op | source)
XLA Modules:
  0.0 30.5 jit_solution(5559976783404109115)
XLA Ops:
  0.6 0.0 copy-start
  0.6 0.0 copy-start.1
  0.7 0.0 copy-start.2
  0.7 0.0 copy-start.3
  0.7 0.0 copy-start.4
  0.7 24.8 %exchange.1 = (f32[72,8,128]{2,1,0:T(8,128)S(1)}, f32[512,2048]{1,0:T(8,128)S(1)}, f32[512,3072]{1,0:T(8,128)S(1)}, bf16[512,3072]{1,0:T(8,128)(2,1)S(1)}, bf16[...) custom-call(s32[12,32]{1,0:T(8,128)} %bitcast.1, ...), custom_call_target="tpu_custom_call" | custom-call | tf_op jit(solution)/shard_map/exchange/pallas_call | solution.py:380
  25.5 0.0 copy-done
  25.5 0.0 copy-done.1
  25.5 0.0 copy-done.2
  25.5 0.0 copy-done.3
  25.5 0.0 copy-done.4
  25.5 5.0 %synapses.1 = (f32[8,512]{1,0:T(8,128)}, f32[8,512]{1,0:T(8,128)}, f32[8,512]{1,0:T(8,128)}, f32[8,512]{1,0:T(8,128)}, f32[512,2048]{1,0:T(8,128)}, /*index=5*/f32[512,3072]{1,0:T(8,128)}) custom-call(f32[72,8,128]{2,1,0:T(8,128)S(1)} %get-tuple-element.15.far_ref, f32[512,2048]{1,0:T(8,128)S(1)} %get-tuple-element.16.local_ref, ...), custom_call_target="tpu_custom_call" | custom-call | tf_op jit(solution)/shard_map/synapses/pallas_call | solution.py:417
Async XLA Ops:
  0.6 24.8 %copy-start = (s32[2,8,512]{2,1,0:T(8,128)S(1)}, s32[2,8,512]{2,1,0:T(8,128)}, u32[]{:S(2)}) copy-start(s32[2,8,512]{2,1,0:T(8,128)} %spikes_ref.1) | copy-start | bytes 98308
  0.6 24.8 %copy-start.1 = (f32[8,512]{1,0:T(8,128)S(1)}, f32[8,512]{1,0:T(8,128)}, u32[]{:S(2)}) copy-start(f32[8,512]{1,0:T(8,128)} %release_ref.1) | copy-start | bytes 49156
  0.7 24.8 %copy-start.2 = (f32[8,512]{1,0:T(8,128)S(1)}, f32[8,512]{1,0:T(8,128)}, u32[]{:S(2)}) copy-start(f32[8,512]{1,0:T(8,128)} %pre_ref.1) | copy-start | bytes 49156
  0.7 24.8 %copy-start.3 = (f32[8,512]{1,0:T(8,128)S(1)}, f32[8,512]{1,0:T(8,128)}, u32[]{:S(2)}) copy-start(f32[8,512]{1,0:T(8,128)} %post_ref.1) | copy-start | bytes 49156
  0.7 24.8 %copy-start.4 = (f32[8,512]{1,0:T(8,128)S(1)}, f32[8,512]{1,0:T(8,128)}, u32[]{:S(2)}) copy-start(f32[8,512]{1,0:T(8,128)} %potential_ref.1) | copy-start | bytes 49156

commit v2 on v1

--- a/solution.py
+++ b/solution.py
@@ -25,7 +25,7 @@
 depletion = 0.5
 
 AXES = (("x", "y", "z"), ("y", "z", "x"), ("z", "x", "y"))
-OFFSETS = (1, 3, 2)
+OFFSETS = (2, 1, 3)
 
 
 def device_of(place):
@@ -188,26 +188,28 @@
     def arrived(ref, sem):
         pltpu.make_async_copy(ref, ref, sem).wait()
 
-    def step_1(kind, place, half):
+    def step_1(kind, place, half, j):
         remote(
             near_ref.at[mine(kind, half)], gathered[kind].at[pl.ds(spots[kind], 2)],
-            send_sem.at[0], recv_1.at[kind], device_of({**place, "c": half}),
+            send_sem.at[0], recv_1.at[kind, j], device_of({**place, "c": half}),
         ).start()
 
-    for offset in OFFSETS:
+    for kind in range(3):
+        step_1(kind, here, 1 - core, 3)
+    for j, offset in enumerate(OFFSETS):
         for kind, (first, _, _) in enumerate(AXES):
             there = moved(here, first, offset)
-            step_1(kind, there, core)
-            step_1(kind, there, 1 - core)
-    for kind in range(3):
-        step_1(kind, here, 1 - core)
-    for flip in range(1, 4):
-        z = here["z"] if flip < 2 else here["z"] + 1 - 2 * lax.rem(here["z"], 2)
-        c = core if flip == 2 else 1 - core
-        remote(
-            near_ref.at[pl.ds(inner * 12, 12)], near_ref.at[pl.ds(inner * 12, 12)],
-            send_sem.at[1], near_recv, device_of({**here, "z": z, "c": c}),
-        ).start()
+            step_1(kind, there, core, j)
+            step_1(kind, there, 1 - core, j)
+    across = {**here, "z": here["z"] + 1 - 2 * lax.rem(here["z"], 2)}
+    across_inner = lax.rem(inner + 2, 4)
+
+    def pass_near(owner, place, number):
+        part = near_ref.at[pl.ds(owner * 12, 12)]
+        remote(part, part, send_sem.at[1], near_recv.at[number], device_of(place)).start()
+
+    pass_near(inner, sibling, 0)
+    pass_near(inner, across, 1)
 
     source_load.wait()
 
@@ -239,6 +241,19 @@
     post_1 = post_ref[...]
     post_2 = (postsyn_trace_decay * post_1 + firing_1) * alive
     left_ref[...] = left_matrix(firing_1, firing_2, post_1, post_2)
+
+    def step_2(kind, j):
+        first, second, _ = AXES[kind]
+        origin = here[first] if j == 3 else lax.rem(here[first] + 4 - OFFSETS[j], 4)
+        part = gathered[kind].at[pl.ds(here[second] * 16 + origin * 4, 4)]
+        arrived(part if j < 3 else part.at[pl.ds(0, 2)], recv_1.at[kind, j])
+        for offset in OFFSETS:
+            remote(
+                part, part, send_sem.at[2], recv_2.at[kind], device_of(moved(here, second, offset))
+            ).start()
+
+    for kind in range(3):
+        step_2(kind, 3)
     weight_loads[0].wait()
 
     @pl.loop(0, OWN // 32)
@@ -249,15 +264,14 @@
         high_ref[rows, :] = big
         low_ref[rows, :] = (value - big.astype(jnp.float32)).astype(jnp.bfloat16)
 
-    for kind, (first, second, _) in enumerate(AXES):
-        arrived(gathered[kind].at[pl.ds(0, 14)], recv_1.at[kind])
-        part = gathered[kind].at[pl.ds(here[second] * 16, 16)]
-        for offset in OFFSETS:
-            remote(
-                part, part, send_sem.at[2], recv_2.at[kind], device_of(moved(here, second, offset))
-            ).start()
-
-    arrived(near_ref.at[pl.ds(0, 36)], near_recv)
+    for j in (1, 2, 0):
+        for kind in range(3):
+            step_2(kind, j)
+
+    arrived(near_ref.at[pl.ds(0, 12)], near_recv.at[1])
+    pass_near(across_inner, sibling, 2)
+    arrived(near_ref.at[pl.ds(0, 12)], near_recv.at[0])
+    arrived(near_ref.at[pl.ds(0, 12)], near_recv.at[2])
     act_1, pre_1, act_2 = (
         jnp.concatenate(
             [near_ref[i * 12 + kind * 4 + h * 2 + b] for i in range(4) for b in range(2) for h in range(2)],
@@ -405,7 +419,7 @@
             *[pltpu.VMEM((48, *TILE), f32)] * 3,
             pltpu.VMEM((80, AREA), bf16),
             pltpu.VMEM((32, AREA), bf16),
-            dma((5,)), dma, dma((2,)), dma, dma((3,)), dma((3,)), dma((3,)), dma, dma((5,)),
+            dma((5,)), dma, dma((2,)), dma((3,)), dma((3, 4)), dma((3,)), dma((3,)), dma, dma((5,)),
         ],
         compiler_params=pltpu.CompilerParams(
             collective_id=0, has_side_effects=True, vmem_limit_bytes=28 << 20

time: 30.6 us -> 29.5 us (0.964)
  Pallas kernels: 29.8 us -> 28.6 us
    pallas_call x1, Pallas kernels: 24.8 us -> 23.7 us  [local(): pl.pallas_call(exchange_kernel, name='exchange', out_shape=(pltpu.VMEM((7...]
where the time goes in v2:
time: 29.5 us; the launch traced here: 29.4 us
  Pallas kernels  28.6 us (97%)
  between operations  0.72 us (2%)
    pallas_call x1, Pallas kernels, local(): pl.pallas_call(exchange_kernel, name='exchange', out_shape=(pltpu.VMEM((7...  23.7 us
    pallas_call x1, Pallas kernels, local(): pl.pallas_call(synapse_kernel, name='synapses', out_shape=(*(jax.ShapeDty...  4.97 us

profile of v2, /device:TPU:1, one launch (start us, length us, event | category | flops | bytes accessed | tf_op | source)
XLA Modules:
  0.0 29.4 jit_solution(15557624254066654056)
XLA Ops:
  0.6 0.0 copy-start
  0.6 0.0 copy-start.1
  0.7 0.0 copy-start.2
  0.7 0.0 copy-start.3
  0.7 0.0 copy-start.4
  0.7 23.7 %exchange.1 = (f32[72,8,128]{2,1,0:T(8,128)S(1)}, f32[512,2048]{1,0:T(8,128)S(1)}, f32[512,3072]{1,0:T(8,128)S(1)}, bf16[512,3072]{1,0:T(8,128)(2,1)S(1)}, bf16[...) custom-call(s32[12,32]{1,0:T(8,128)} %bitcast.1, ...), custom_call_target="tpu_custom_call" | custom-call | tf_op jit(solution)/shard_map/exchange/pallas_call | solution.py:394
  24.4 0.0 copy-done
  24.4 0.0 copy-done.1
  24.4 0.0 copy-done.2
  24.4 0.0 copy-done.3
  24.4 0.0 copy-done.4
  24.4 5.0 %synapses.1 = (f32[8,512]{1,0:T(8,128)}, f32[8,512]{1,0:T(8,128)}, f32[8,512]{1,0:T(8,128)}, f32[8,512]{1,0:T(8,128)}, f32[512,2048]{1,0:T(8,128)}, /*index=5*/f32[512,3072]{1,0:T(8,128)}) custom-call(f32[72,8,128]{2,1,0:T(8,128)S(1)} %get-tuple-element.15.far_ref, f32[512,2048]{1,0:T(8,128)S(1)} %get-tuple-element.16.local_ref, ...), custom_call_target="tpu_custom_call" | custom-call | tf_op jit(solution)/shard_map/synapses/pallas_call | solution.py:431
Async XLA Ops:
  0.6 23.7 %copy-start = (s32[2,8,512]{2,1,0:T(8,128)S(1)}, s32[2,8,512]{2,1,0:T(8,128)}, u32[]{:S(2)}) copy-start(s32[2,8,512]{2,1,0:T(8,128)} %spikes_ref.1) | copy-start | bytes 98308
  0.6 23.7 %copy-start.1 = (f32[8,512]{1,0:T(8,128)S(1)}, f32[8,512]{1,0:T(8,128)}, u32[]{:S(2)}) copy-start(f32[8,512]{1,0:T(8,128)} %release_ref.1) | copy-start | bytes 49156
  0.7 23.7 %copy-start.2 = (f32[8,512]{1,0:T(8,128)S(1)}, f32[8,512]{1,0:T(8,128)}, u32[]{:S(2)}) copy-start(f32[8,512]{1,0:T(8,128)} %pre_ref.1) | copy-start | bytes 49156
  0.7 23.7 %copy-start.3 = (f32[8,512]{1,0:T(8,128)S(1)}, f32[8,512]{1,0:T(8,128)}, u32[]{:S(2)}) copy-start(f32[8,512]{1,0:T(8,128)} %post_ref.1) | copy-start | bytes 49156
  0.7 23.7 %copy-start.4 = (f32[8,512]{1,0:T(8,128)S(1)}, f32[8,512]{1,0:T(8,128)}, u32[]{:S(2)}) copy-start(f32[8,512]{1,0:T(8,128)} %potential_ref.1) | copy-start | bytes 49156
